TPU v7x, 256 devices: a 2x2x32 block of a 4x8x32 slice. The times are simulated.
256 devices in a mesh: groups: 4 (over y, x), expert: 64 (over z, core).
Axes of the slice: x: 2, y: 2, z: 32, core: 2. Of those that a mesh axis runs over, the one named last changes fastest.
The devices are a block of a 4x8x32 slice.
Arguments:
- tokens: bfloat16 [4096, 6144], P(('groups', 'expert')), parts along dimension 0, may hold values from -6 to 6
- route_ids: int32 [4096, 2], P(('groups', 'expert')), parts along dimension 0, may hold values from 0 to 7, all different within a row; in each aligned block of 16 rows (0 to 15, 16 to 31, ...) at most 6 rows name the same one
- route_logits: float32 [4096, 2], P(('groups', 'expert')), parts along dimension 0, may hold values from -6 to 6
- old_place: int32 [64], replicated, may hold values from 0 to 63, each once
- new_place: int32 [64], replicated, may hold values from 0 to 63, each once
- held_gate: bfloat16 [256, 6144, 128], P(('groups', 'expert')), parts along dimension 0, may hold values from -0.078125 to 0.078125
- held_up: bfloat16 [256, 6144, 128], P(('groups', 'expert')), parts along dimension 0, may hold values from -0.078125 to 0.078125
- held_down: bfloat16 [256, 6144, 128], P(('groups', 'expert')), parts along dimension 0, may hold values from -0.1875 to 0.1875
Outputs:
- moe_output: bfloat16 [4096, 6144], P(('groups', 'expert')), parts along dimension 0
- moved_gate: bfloat16 [256, 6144, 128], P(('groups', 'expert')), parts along dimension 0
- moved_up: bfloat16 [256, 6144, 128], P(('groups', 'expert')), parts along dimension 0
- moved_down: bfloat16 [256, 6144, 128], P(('groups', 'expert')), parts along dimension 0
There are 4 independent parts, one for each index of `groups`. A program takes and returns all parts, laid end to end along the dimension named above; an argument that names none is the same for every part. Nothing has to cross between parts.
Inputs may be any that keep to these rules, and one draw needn't show every extreme that they name: `route_ids`: within the rows of one device (aligned blocks of 16 rows) no expert is named by more than 6 rows, a bound that some block reaches; the two ids of a row differ. `old_place`: each device appears once. `new_place`: each device appears once.
All inputs are finite; a program needn't handle non-finite values.
Results may differ from a plain program's by a relative error of at most 0.0058.
Values may be sent and summed in bfloat16 or wider, within the bound.
A program may use at most 128 MiB of HBM per device.

v0:
```python
import jax
import jax.numpy as jnp
from jax import lax
from jax.sharding import PartitionSpec as P

EXPERTS = 8
CAP = 6


def in_one_piece(arrays, axis, split_dim, concat_dim, along):
    both = jnp.concatenate(arrays, axis=along)
    out, at, gathered = (
        lax.all_to_all(both, axis, split_axis=split_dim, concat_axis=concat_dim, tiled=True),
        0,
        [],
    )
    for a in arrays:
        gathered.append(lax.slice_in_dim(out, at, at + a.shape[along], axis=along))
        at += a.shape[along]
    return tuple(gathered)


def inverse_of(placement, device_ids):
    return jnp.sum(
        jnp.where(placement[:, None] == device_ids[None, :], device_ids[:, None], 0), axis=0
    )


def per_device(
    tokens, route_ids, route_logits, old_place, new_place, held_gate, held_up, held_down
):
    devices = lax.axis_size("expert")
    width = tokens.shape[1]
    tok_rows = tokens.shape[0]
    device_ids = jnp.arange(devices, dtype=jnp.int32)
    slot_new_at = inverse_of(new_place, device_ids)
    slot_old_at = inverse_of(old_place, device_ids)
    source_of = jnp.take(old_place, slot_new_at)
    pieces = in_one_piece((held_gate, held_up, held_down), "expert", 1, 0, 2)
    reordered = (
        jnp.take(pieces[0], source_of, axis=0),
        jnp.take(pieces[1], source_of, axis=0),
        jnp.take(pieces[2], source_of, axis=0),
    )
    migrated = in_one_piece((reordered[0], reordered[1], reordered[2]), "expert", 0, 1, 2)
    w_gate, w_up, w_down = (held_gate, held_up, held_down)
    blocks = devices // EXPERTS
    expert_at = slot_old_at // blocks
    expert_ids = jnp.arange(EXPERTS, dtype=jnp.int32)
    route_hits = route_ids[:, :, None] == expert_ids[None, None, :]
    routed = jnp.any(route_hits, axis=1).astype(jnp.int32)
    position = jnp.cumsum(routed, axis=0) - 1
    bucket_ids = jnp.arange(CAP, dtype=jnp.int32)
    bucket_table = (routed[:, :, None] == 1) & (position[:, :, None] == bucket_ids[None, None, :])
    picker = bucket_table.reshape(tok_rows, EXPERTS * CAP).astype(jnp.bfloat16)
    buckets = lax.dot_general(
        picker, tokens, (((0,), (0,)), ((), ())), preferred_element_type=jnp.float32
    )
    buckets = buckets.astype(jnp.bfloat16).reshape(EXPERTS, CAP, width)
    outgoing = jnp.take(buckets, expert_at, axis=0)
    incoming = lax.all_to_all(outgoing, "expert", split_axis=0, concat_axis=0, tiled=True)
    sources = incoming.shape[0]
    count = incoming.shape[1]
    stacked = incoming.reshape(sources * count, width)
    gate_value = jnp.dot(stacked, w_gate[0], preferred_element_type=jnp.float32)
    up_value = jnp.dot(stacked, w_up[0], preferred_element_type=jnp.float32)
    hidden = (jax.nn.silu(gate_value) * up_value).astype(jnp.bfloat16)
    partial_value = lax.dot_general(
        hidden, w_down[0], (((1,), (1,)), ((), ())), preferred_element_type=jnp.float32
    )
    partial_value = partial_value.astype(jnp.bfloat16).reshape(sources, count, width)
    returned = lax.all_to_all(partial_value, "expert", split_axis=0, concat_axis=0, tiled=True)
    membership = (expert_at[None, :] == expert_ids[:, None]).astype(jnp.bfloat16)
    expert_sum = jnp.dot(
        membership, returned.reshape(devices, CAP * width), preferred_element_type=jnp.float32
    )
    expert_sum = expert_sum.reshape(EXPERTS * CAP, width)
    token_slot = jnp.take_along_axis(position, route_ids, axis=1)
    row_index = route_ids * CAP + token_slot
    selected = jnp.take(expert_sum, row_index.reshape(-1), axis=0).reshape(tok_rows, 2, width)
    first_weight = 1.0 / (1.0 + jnp.exp(route_logits[:, 1] - route_logits[:, 0]))
    second_weight = 1.0 / (1.0 + jnp.exp(route_logits[:, 0] - route_logits[:, 1]))
    weights = jnp.stack([first_weight, second_weight], axis=1)
    combined = jnp.sum(weights[:, :, None] * selected, axis=1).astype(jnp.bfloat16)
    return (combined, migrated[0], migrated[1], migrated[2])


def solution(mesh):
    placed = (
        P(("groups", "expert"), None),
        P(("groups", "expert"), None),
        P(("groups", "expert"), None),
        P(),
        P(),
        P(("groups", "expert"), None, None),
        P(("groups", "expert"), None, None),
        P(("groups", "expert"), None, None),
    )
    return jax.shard_map(
        per_device,
        mesh=mesh,
        in_specs=placed,
        out_specs=(
            P(("groups", "expert"), None),
            P(("groups", "expert"), None, None),
            P(("groups", "expert"), None, None),
            P(("groups", "expert"), None, None),
        ),
        check_vma=False,
    )
```

profile of v0, /device:TPU:46, one launch (start us, length us, event | category | flops | bytes accessed | tf_op | source)
XLA Modules:
  0.0 2042.5 jit_solution(15707181968553112017)
XLA Ops:
  3.1 3.6 gather_fusion
  6.7 6.3 broadcast_select_fusion
  12.9 35.1 %all-to-all-start = ((bf16[64,6,6144]{2,1,0:T(8,128)(2,1)}), bf16[64,6,6144]{2,1,0:T(8,128)(2,1)}, u32[]{:S(2)}, u32[]{:S(2)}) async-start(bf16[64,6,6144]{2,1,0:T(8,128)(2,1)} %broadcast_select_fusion), calls=%async_computation | async-start | bytes 12582912 | tf_op jit(solution)/shard_map/all_to_all | solution.py:61
  50.1 88.7 %copy.106 = bf16[1,6144,384]{2,0,1:T(2,128)(2,1)} copy(bf16[1,6144,384]{2,1,0:T(8,128)(2,1)S(1)} %pad_maximum_fusion) | data formatting | bytes 9437184 | tf_op jit(solution)/shard_map/concatenate | solution.py:11
  139.2 101.9 %reduce = bf16[6144,384]{1,0:T(8,128)(2,1)} reduce(bf16[6144,1,384]{2,1,0:T(2,128)(2,1)} %bitcast.53, bf16[]{:T(256)} %broadcast.270), dimensions={1}, to_apply=%bitcast.52.reduce_sub_computation | reduce | bytes 9437186
  241.1 10.5 reshape.275
  251.6 355.0 %all-to-all-done = bf16[64,6,6144]{2,1,0:T(8,128)(2,1)} async-done(((bf16[64,6,6144]{2,1,0:T(8,128)(2,1)}), bf16[64,6,6144]{2,1,0:T(8,128)(2,1)}, u32[]{:S(2)}, u32[]{:S(2)}) %all-to-all-start) | async-done | bytes 4718624 | tf_op jit(solution)/shard_map/all_to_all | solution.py:61
  606.6 7.3 all-to-all-start.2
  614.0 7.8 reshape.202
  621.8 4.2 fusion.3
  626.0 9.5 convolution_convert_fusion
  635.6 7.8 reshape.203
  643.3 394.6 %all-to-all-done.2 = bf16[64,2,18432]{2,1,0:T(2,128)(2,1)} async-done(((bf16[64,2,18432]{2,1,0:T(2,128)(2,1)}), bf16[64,2,18432]{2,1,0:T(2,128)(2,1)}, u32[]{:S(2)}, u32[]{:S(2)}) %all-to-all-start.2) | async-done | bytes 4718624 | tf_op jit(solution)/shard_map/all_to_all | solution.py:13
  1037.9 7.6 all-to-all-start.1
  1046.4 20.2 reshape.276
  1066.7 4.5 copy.103
  1071.2 2.5 fusion.32
  1076.8 3.3 gather_fusion.6
  1082.2 2.5 pad_maximum_fusion.1
  1084.6 519.6 %all-to-all-done.1 = bf16[64,6,6144]{2,1,0:T(8,128)(2,1)} async-done(((bf16[64,6,6144]{2,1,0:T(8,128)(2,1)}), bf16[64,6,6144]{2,1,0:T(8,128)(2,1)}, u32[]{:S(2)}, u32[]{:S(2)}) %all-to-all-start.1) | async-done | bytes 4718624 | tf_op jit(solution)/shard_map/all_to_all | solution.py:72
  1604.2 7.6 all-to-all-start.3
  1613.3 5.5 copy.104
  1621.1 414.6 %all-to-all-done.3 = bf16[64,96,384]{2,1,0:T(8,128)(2,1)} async-done(((bf16[64,96,384]{2,1,0:T(8,128)(2,1)}), bf16[64,96,384]{2,1,0:T(8,128)(2,1)}, u32[]{:S(2)}, u32[]{:S(2)}) %all-to-all-start.3) | async-done | bytes 4718624 | tf_op jit(solution)/shard_map/all_to_all | solution.py:13
  2035.7 4.7 fusion.31
  (65 shorter events, 16.6 us)
Async XLA Ops:
  0.6 1.9 copy-start
  12.9 35.1 %copy-start.3 = (bf16[1,6144,128]{2,1,0:T(8,128)(2,1)S(1)}, bf16[1,6144,128]{2,1,0:T(8,128)(2,1)}, u32[]{:S(2)}) copy-start(bf16[1,6144,128]{2,1,0:T(8,128)(2,1)} %param.17) | copy-start | bytes 4718596
  12.9 35.1 %copy-start.4 = (bf16[1,6144,128]{2,1,0:T(8,128)(2,1)S(1)}, bf16[1,6144,128]{2,1,0:T(8,128)(2,1)}, u32[]{:S(2)}) copy-start(bf16[1,6144,128]{2,1,0:T(8,128)(2,1)} %param.16) | copy-start | bytes 4718596
  12.9 593.7 %all-to-all-start = ((bf16[64,6,6144]{2,1,0:T(8,128)(2,1)}), bf16[64,6,6144]{2,1,0:T(8,128)(2,1)}, u32[]{:S(2)}, u32[]{:S(2)}) async-start(bf16[64,6,6144]{2,1,0:T(8,128)(2,1)} %broadcast_select_fusion), calls=%async_computation | async-start | bytes 12582912 | tf_op jit(solution)/shard_map/all_to_all | solution.py:61
  606.6 431.2 %all-to-all-start.2 = ((bf16[64,2,18432]{2,1,0:T(2,128)(2,1)}), bf16[64,2,18432]{2,1,0:T(2,128)(2,1)}, u32[]{:S(2)}, u32[]{:S(2)}) async-start(bf16[64,2,18432]{2,1,0:T(2,128)(2,1)} %reshape.275), calls=%async_computation.2 | async-start | bytes 9437184 | tf_op jit(solution)/shard_map/all_to_all | solution.py:13
  643.3 402.2 %copy-start.7 = (s32[64]{0:T(128)S(1)}, s32[64]{0:T(128)}, u32[]{:S(2)}) copy-start(s32[64]{0:T(128)} %param.14) | copy-start | bytes 772
  643.3 402.3 %copy-start.2 = (s32[64]{0:T(128)S(1)}, s32[64]{0:T(128)}, u32[]{:S(2)}) copy-start(s32[64]{0:T(128)} %param.13) | copy-start | bytes 772
  1037.9 566.3 %all-to-all-start.1 = ((bf16[64,6,6144]{2,1,0:T(8,128)(2,1)}), bf16[64,6,6144]{2,1,0:T(8,128)(2,1)}, u32[]{:S(2)}, u32[]{:S(2)}) async-start(bf16[64,6,6144]{2,1,0:T(8,128)(2,1)} %reshape.203), calls=%async_computation.1 | async-start | bytes 12582912 | tf_op jit(solution)/shard_map/all_to_all | solution.py:72
  1084.6 527.2 %copy-start.5 = (s32[16,2]{0,1:T(2,128)S(1)}, s32[16,2]{0,1:T(2,128)}, u32[]{:S(2)}) copy-start(s32[16,2]{0,1:T(2,128)} %param.11) | copy-start | bytes 388
  1604.2 431.5 %all-to-all-start.3 = ((bf16[64,96,384]{2,1,0:T(8,128)(2,1)}), bf16[64,96,384]{2,1,0:T(8,128)(2,1)}, u32[]{:S(2)}, u32[]{:S(2)}) async-start(bf16[64,96,384]{2,1,0:T(8,128)(2,1)} %pad_maximum_fusion.1), calls=%async_computation.3 | async-start | bytes 9437184 | tf_op jit(solution)/shard_map/all_to_all | solution.py:13
  1612.0 1.2 copy-start.6
  2035.7 6.5 copy-start.1
where the time goes:
time: 2050 us; the launch traced here: 2040 us
  waiting for transfers between devices  1680 us (82%)
  local copies, waits for them, and re-layouts  167 us (8%)
  other arithmetic  118 us (6%)
  starting transfers between devices  57.6 us (3%)
    all_to_all x2, waiting for transfers between devices, in_one_piece(): lax.all_to_all(both, axis, split_axis=split_dim, concat_axis=concat_dim,...  809 us
    all_to_all x1, waiting for transfers between devices, per_device(): lax.all_to_all(partial_value, 'expert', split_axis=0, concat_axis=0, tile...  520 us
    all_to_all x1, waiting for transfers between devices, per_device(): lax.all_to_all(outgoing, 'expert', split_axis=0, concat_axis=0, tiled=True)  355 us
    unnamed x1, other arithmetic  102 us
    concatenate x1, local copies, waits for them, and re-layouts, in_one_piece(): both = jnp.concatenate(arrays, axis=along)  88.7 us
    unnamed x21, local copies, waits for them, and re-layouts  41.2 us
  transfers between devices with their start and end apart: 4, of which 4 were waited for; matrix products, arithmetic and copies ran while one was open for 14% of the time, Pallas kernels for 0%

commit v1 on v0

v1 whole, which is shorter than its diff:
```python
import functools

import jax
import jax.numpy as jnp
from jax import lax
from jax.experimental import pallas as pl
from jax.experimental.pallas import tpu as pltpu
from jax.sharding import PartitionSpec as P

EXPERTS = 8
LANES = 128
PIECES = 4
PACKETS = 12
LAG = 2
LANDINGS = 4
SENDS = 3
STAGES = 4
STEPS = (104, 110, 116, 122, 128, 134, 146)
LIMIT = STEPS[-1]
ROUNDS = 48
BETA = 2.0 * 0.6931472
RISE = 4.0 ** (1.0 / (ROUNDS - 1))
FALL = 0.02 ** (1.0 / (ROUNDS - 1))
TRADES = 16
MESH = pl.DeviceIdType.MESH


def column(row, size):
    r = lax.broadcasted_iota(jnp.int32, (size, size), 0)
    c = lax.broadcasted_iota(jnp.int32, (size, size), 1)
    return jnp.sum(jnp.where(r == c, jnp.broadcast_to(row, (size, size)), 0), axis=1, keepdims=True)


def pick(mask, values):
    return jnp.sum(jnp.where(mask, values, 0.0), axis=0, keepdims=True)


class Plan:
    def __init__(self, chips, chip, old_ref, new_ref, table_ref, choice_ref, fixed, live, small, sched):
        self.chips, self.chip, self.slots = chips, chip, 2 * chips
        self.old_ref, self.new_ref, self.table_ref, self.choice_ref = old_ref, new_ref, table_ref, choice_ref
        self.fixed, self.live, self.small, self.sched = fixed, live, small, sched
        self.rows = sched.shape[0]

    def lanes(self):
        return lax.broadcasted_iota(jnp.int32, (self.slots, LANES), 1)

    def start(self):
        chips, slots = self.chips, self.slots
        old, new = column(self.old_ref[...], slots), column(self.new_ref[...], slots)
        src, dst = old // 2, new // 2
        lanes = self.lanes()
        upward = lanes < chips
        spot = jnp.where(upward, lanes, lanes - chips)
        ahead = dst - src
        ahead = jnp.where(ahead < 0, ahead + chips, ahead)
        back = jnp.where(ahead == 0, 0, chips - ahead)
        origin = jnp.where(upward, src, jnp.where(src == 0, 0, chips - src))
        gone = spot - origin
        gone = jnp.where(gone < 0, gone + chips, gone)
        length = jnp.where(upward, ahead, back)
        here = (lanes < slots) & (gone < length)
        left = jnp.where(here, length - gone, 0).astype(jnp.float32)
        first = here & (gone == 0)
        ids = lax.broadcasted_iota(jnp.int32, (slots, LANES), 0).astype(jnp.float32)
        key = jnp.where(here, left * slots + ids, -3.0)
        one, wrapped = pltpu.roll(key, 1, 1), pltpu.roll(key, LANES - (chips - 1), 1)
        behind = jnp.where((lanes == 0) | (lanes == chips), wrapped, one)
        self.fixed[0] = jnp.where(here, 1.0, 0.0)
        self.fixed[1] = key
        self.fixed[2] = jnp.where(here & ~first, behind, -2.0)
        self.fixed[3] = jnp.where(first, 1.0, 0.0)
        ups = ahead.astype(jnp.float32)
        self.live[0] = jnp.broadcast_to(jnp.clip(0.5 + (0.5 * chips - ups) * 0.25, 0.0, 1.0), (slots, LANES))
        self.small[...] = jnp.full(self.small.shape, -1.0, jnp.float32)
        self.sched[...] = jnp.full(self.sched.shape, -1.0, jnp.float32)

    def price(self, x, total, beta):
        on = self.fixed[0]
        share = jnp.where(self.lanes() < self.chips, x, total - x)
        load = jnp.sum(share * on, axis=0, keepdims=True)
        top = jnp.max(load, axis=1, keepdims=True)
        lane = lax.broadcasted_iota(jnp.int32, (1, LANES), 1)
        return jnp.where(lane < self.slots, jnp.exp(beta * (load - top)), 0.0)

    def descend(self, i):
        i = jnp.asarray(i, jnp.int32).astype(jnp.float32) * jnp.ones((1, 1), jnp.float32)
        beta = BETA * jnp.exp(i * jnp.log(jnp.float32(RISE)))
        step = jnp.exp(i * jnp.log(jnp.float32(FALL)))
        x, on = self.live[0], self.fixed[0]
        price = self.price(x, 1.0, beta)
        total = jnp.sum(price, axis=1, keepdims=True)
        gain = jnp.sum(jnp.where(self.lanes() < self.chips, -on, on) * price, axis=1, keepdims=True)
        self.live[0] = jnp.clip(x + step * (gain / total), 0.0, 1.0)

    def settle(self):
        self.live[0] = jnp.floor(self.live[0] * PACKETS + 0.5)

    def trade(self):
        u, on = self.live[0], self.fixed[0]
        price = self.price(u, float(PACKETS), 0.6931472) * on
        upward = self.lanes() < self.chips
        lower = jnp.sum(jnp.where(upward, -0.5, 1.0) * price, axis=1, keepdims=True)
        higher = jnp.sum(jnp.where(upward, 1.0, -0.5) * price, axis=1, keepdims=True)
        units = u[:, 0:1]
        moves = jnp.sum(on, axis=1, keepdims=True) > 0
        lower = jnp.where(moves & (units > 0), lower, 1e9)
        higher = jnp.where(moves & (units < PACKETS), higher, 1e9)
        best = jnp.minimum(lower, higher)
        least = jnp.min(best, axis=0, keepdims=True)
        ids = lax.broadcasted_iota(jnp.int32, (self.slots, 1), 0).astype(jnp.float32)
        chosen = jnp.min(jnp.where(best == least, ids, 1e9), axis=0, keepdims=True)
        turn = (ids == chosen) & (least < 0)
        self.live[0] = u + jnp.where(turn, jnp.where(lower < higher, -1.0, 1.0), 0.0)

    def load(self):
        u = self.live[0]
        self.live[1] = self.fixed[3] * jnp.where(self.lanes() < self.chips, u, PACKETS - u)

    def send(self, t):
        key, before, count, came = self.fixed[1], self.fixed[2], self.live[1], self.small[0]
        ready = count > 0
        best = jnp.max(jnp.where(ready, key, -1.0), axis=0, keepdims=True)
        self.live[1] = (
            count - jnp.where(ready & (key == best), 1.0, 0.0) + jnp.where(before == came[0:1], 1.0, 0.0)
        )
        wide = jnp.broadcast_to(best, came.shape)
        slot = jnp.where(wide < 0, -1.0, wide - self.slots * jnp.floor(wide / self.slots))
        self.sched[pl.ds(t, 1), :] = slot[0:1]
        self.small[1] = jnp.where(wide >= 0, jnp.asarray(t, jnp.int32).astype(jnp.float32), self.small[1])
        one, wrapped = pltpu.roll(wide, 1, 1), pltpu.roll(wide, LANES - (self.chips - 1), 1)
        lane = lax.broadcasted_iota(jnp.int32, came.shape, 1)
        self.small[0] = jnp.where((lane == 0) | (lane == self.chips), wrapped, one)

    def held(self):
        ids = lax.broadcasted_iota(jnp.int32, (self.slots, 1), 0).astype(jnp.float32)
        old = column(self.old_ref[...], self.slots)
        return [pick(old == 2 * self.chip + q, ids) for q in range(2)]

    def finish(self):
        chips, chip, slots, rows = self.chips, self.chip, self.slots, self.rows
        tall = -(-LIMIT // 8) * 8
        left = self.live[1] + jnp.where(self.fixed[2] == self.small[0, 0:1], 1.0, 0.0)
        used = jnp.max(self.small[1]) + 1.0
        choice = jnp.int32(0)
        for s in STEPS:
            choice = choice + jnp.where(used > s, 1, 0)
        self.choice_ref[0] = jnp.where(jnp.max(left) > 0, len(STEPS), choice)

        table = self.sched[...]
        turned = jnp.concatenate(
            [jnp.transpose(table[k * LANES:(k + 1) * LANES]) for k in range(rows // LANES)], axis=1
        )
        table = table[:tall]
        lane = lax.broadcasted_iota(jnp.int32, (tall, LANES), 1)
        line = lax.broadcasted_iota(jnp.int32, (LANES, rows), 0)
        early = lax.broadcasted_iota(jnp.int32, (tall, rows), 0)
        late = lax.broadcasted_iota(jnp.int32, (tall, rows), 1)
        mirror = jnp.where(chip == 0, 0, chips - chip)
        ends = (
            (chip, jnp.where(chip == 0, chips - 1, chip - 1)),
            (chips + mirror, chips + jnp.where(mirror == 0, chips - 1, mirror - 1)),
        )
        ids = lax.broadcasted_iota(jnp.int32, (slots, 1), 0).astype(jnp.float32)
        old, new = column(self.old_ref[...], slots), column(self.new_ref[...], slots)
        units = self.live[0][:, 0:1]

        held = self.held()
        due = [pick(new == 2 * chip + q, ids) for q in range(2)]
        place = lax.broadcasted_iota(jnp.int32, (1, LANES), 1).astype(jnp.float32)
        base = 2.0 * PACKETS
        sends, found = [], [[], []]
        for way, (mine, theirs) in enumerate(ends):
            out = jnp.sum(jnp.where(lane == mine, table, 0.0), axis=1, keepdims=True)
            got = jnp.sum(jnp.where(lane == theirs, table, 0.0), axis=1, keepdims=True)
            out_row = jnp.sum(jnp.where(line == mine, turned, 0.0), axis=0, keepdims=True)
            got_row = jnp.sum(jnp.where(line == theirs, turned, 0.0), axis=0, keepdims=True)
            out_rank = jnp.sum(jnp.where((out_row == out) & (late < early), 1.0, 0.0), axis=1, keepdims=True)
            got_rank = jnp.sum(jnp.where((got_row == got) & (late < early), 1.0, 0.0), axis=1, keepdims=True)
            rank_row = jnp.sum(jnp.where((got_row == got) & (early < late), 1.0, 0.0), axis=0, keepdims=True)
            spots = base + 2.0 * late.astype(jnp.float32) + way
            index = jnp.sum(jnp.where((got_row == out) & (rank_row == out_rank), spots, 0.0), axis=1, keepdims=True)
            for q in range(2):
                skipped = pick(ids == held[q], units) if way else 0.0
                index = jnp.where(out == held[q], q * PACKETS + skipped + out_rank, index)
            sends.append(jnp.where(out < 0, 0.0, index))
            here = base + 2.0 * lax.broadcasted_iota(jnp.int32, (tall, 1), 0).astype(jnp.float32) + way
            for q in range(2):
                wanted = place - (pick(ids == due[q], units) if way else 0.0)
                found[q].append(jnp.sum(jnp.where((got == due[q]) & (got_rank == wanted), here, 0.0), axis=0, keepdims=True))
        both = jnp.where(lane == 0, sends[0], jnp.where(lane == 1, sends[1], 0.0))
        self.table_ref[pl.ds(0, LIMIT), :] = both[:LIMIT].astype(jnp.int32)
        for q in range(2):
            source = pick(ids == due[q], old.astype(jnp.float32)).astype(jnp.int32)
            packets = jnp.where(place < pick(ids == due[q], units), found[q][0], found[q][1])
            stays = (source % 2).astype(jnp.float32) * PACKETS + place
            packets = jnp.where(source // 2 == chip, stays, packets)
            self.table_ref[pl.ds(LIMIT + q, 1), :] = jnp.where(place < PACKETS, packets, 0.0).astype(jnp.int32)


def token_kernel(
    chips, experts, blocks,
    old_ref, new_ref, tokens, ids_ref, logits_ref, gate, up, down,
    result, table, choice, mate_half,
    rows_all, gate_up, downs, hidden, inbox, outbox, fixed, live, small, sched,
    own_sems, pair_sems, half_sems, ag_send, ag_recv, rs_send, rs_recv,
):
    half = chips // 2
    count, width = tokens.shape
    feats = gate.shape[1]
    cols = width // PIECES
    tail = rows_all.shape[2] - width
    me = lax.axis_index("expert")
    chip, core = me // 2, me % 2
    mate = {"expert": me + 1 - 2 * core}
    ways = ({"expert": ((chip + 1) % chips) * 2 + core}, {"expert": ((chip + chips - 1) % chips) * 2 + core})
    plan = Plan(chips, chip, old_ref, new_ref, table, choice, fixed, live, small, sched)

    lane = lax.broadcasted_iota(jnp.int32, (count, tail), 1)
    first, second = (column(logits_ref[i:i + 1, :], count) for i in range(2))
    expert0, expert1 = (column(ids_ref[i:i + 1, :], count) for i in range(2))
    weight0 = 1.0 / (1.0 + jnp.exp(second - first))
    weight1 = 1.0 / (1.0 + jnp.exp(first - second))
    which = lane % experts
    value = jnp.where(which == expert0, weight0, jnp.where(which == expert1, weight1, 0.0))
    high = value.astype(jnp.bfloat16).astype(jnp.float32)
    middle = (value - high).astype(jnp.bfloat16).astype(jnp.float32)
    low = value - high - middle
    part = lane // experts
    routed = jnp.where(part == 0, high, jnp.where(part == 1, middle, jnp.where(part == 2, low, 0.0)))
    rows_all[chip, :, width:] = routed.astype(jnp.bfloat16)

    rows_all[chip, :, pl.ds(0, width)] = tokens[...]
    loads = []
    for a, (array, target) in enumerate(
        (
            (gate, gate_up.at[core, :, pl.ds(0, feats)]),
            (up, gate_up.at[core, :, pl.ds(feats, feats)]),
            (down, downs.at[core]),
        )
    ):
        kept = pltpu.make_async_copy(array, target, own_sems.at[a])
        kept.start()
        given = pltpu.make_async_remote_copy(
            src_ref=array, dst_ref=target, send_sem=pair_sems.at[0, a], recv_sem=pair_sems.at[1, a],
            device_id=mate, device_id_type=MESH,
        )
        loads.append((kept, given))

    barrier = pltpu.get_barrier_semaphore()
    for other in (mate,) + ways:
        pl.semaphore_signal(barrier, inc=1, device_id=other, device_id_type=MESH)
    pl.semaphore_wait(barrier, 3)

    def span(p):
        return pl.ds(p * cols, cols + (tail if p == PIECES - 1 else 0))

    def around(offset):
        return lax.rem(chip + offset + 2 * chips, chips)

    def pass_on(way, step, p):
        at = around(1 - step if way == 0 else step - 1)
        view = rows_all.at[at, :, span(p)]
        return pltpu.make_async_remote_copy(
            src_ref=view, dst_ref=view, send_sem=ag_send.at[way, step % 2, p], recv_sem=ag_recv.at[way, step % 2, p],
            device_id=ways[way], device_id_type=MESH,
        )

    def landed(way, step, p):
        at = around(-step if way == 0 else step)
        view = rows_all.at[at, :, span(p)]
        return pltpu.make_async_remote_copy(
            src_ref=view, dst_ref=view, send_sem=ag_send.at[way, step % 2, p], recv_sem=ag_recv.at[way, step % 2, p],
            device_id=ways[way], device_id_type=MESH,
        )

    def shares(way, p):
        return (p < PIECES // 2) == (way == 0)

    def group_rows(g, p):
        view = pl.ds(p * cols, cols)
        if isinstance(g, int) and g in (0, half):
            return rows_all[around(g), :, view]
        return jnp.concatenate([rows_all[around(-g), :, view], rows_all[around(g), :, view]], axis=0)

    def project(g, p, sums):
        x = group_rows(g, p)
        return [
            sums[q] + jnp.dot(x, gate_up[q, pl.ds(p * cols, cols), :], preferred_element_type=jnp.float32)
            for q in range(2)
        ]

    def activate(g, sums):
        for q in range(2):
            g_val, u_val = sums[q][:, :feats], sums[q][:, feats:]
            h = (g_val / (1.0 + jnp.exp(-g_val)) * u_val).astype(jnp.bfloat16)
            if isinstance(g, int) and g in (0, half):
                hidden[around(g), q] = h
            else:
                hidden[around(-g), q] = h[:count]
                hidden[around(g), q] = h[count:]

    def zeros(g):
        m = count if isinstance(g, int) and g in (0, half) else 2 * count
        return [jnp.zeros((m, 2 * feats), jnp.float32) for _ in range(2)]

    def whole(g):
        sums = zeros(g)
        for p in range(PIECES):
            sums = project(g, p, sums)
        activate(g, sums)

    for p in range(PIECES):
        for way in range(2):
            pass_on(way, 1, p).start()
    for _, given in loads:
        given.start()

    def chore(step, p):
        at = 4 * (step - 3) + p

        @pl.when(step < 7)
        def _():
            for i in range(ROUNDS // 16):
                plan.descend(at * (ROUNDS // 16) + i)

            if p == PIECES - 1:

                @pl.when(step == 6)
                def _():
                    plan.settle()

        @pl.when((step >= 7) & (step < 9))
        def _():
            for i in range(TRADES // 8):
                plan.trade()

            if p == PIECES - 1:

                @pl.when(step == 8)
                def _():
                    plan.load()

        @pl.when(step >= 9)
        def _():
            for i in range(LIMIT // 24):
                plan.send((at - 24) * (LIMIT // 24) + i)

    def chores():
        def descend(i, carry):
            plan.descend(i)
            return carry

        def trade(i, carry):
            plan.trade()
            return carry

        def send(i, carry):
            plan.send(i)
            return carry

        lax.fori_loop(0, ROUNDS, descend, 0)
        plan.settle()
        lax.fori_loop(0, TRADES, trade, 0)
        plan.load()
        lax.fori_loop(0, LIMIT // 24 * 24, send, 0)

    def ag_step(step, g, reuse, last, between=None):
        sums = None if g is None else zeros(g)
        for p in range(PIECES):
            for way in range(2):
                landed(way, step, p).wait_recv()
            for way in range(2):
                if not last or shares(way, p):
                    if reuse:
                        pass_on(way, step - 1, p).wait_send()
                    pass_on(way, step + 1, p).start()
            if g is not None:
                sums = project(g, p, sums)
            if between is not None:
                between(step, p)
        if g is not None:
            activate(g, sums)

    def weights_in():
        for kept, given in loads:
            kept.wait()
            given.wait()
        for copy in mate_copies():
            copy.start()

    def mate_copies():
        rows = width // 2
        near = pl.ds(core * rows, rows)
        views = (
            gate_up.at[1 - core, near, pl.ds(0, feats)],
            gate_up.at[1 - core, near, pl.ds(feats, feats)],
            downs.at[1 - core, near, :],
        )
        return [pltpu.make_async_copy(v, mate_half.at[a], half_sems.at[a]) for a, v in enumerate(views)]

    steady = half - 4 == 12
    plan.start()
    if not steady:
        chores()
    for step in range(1, min(3, half)):
        if step == 2:
            weights_in()
        ag_step(step, None if step == 1 else 0, step > 1, step == half - 1)
    if half > 4:

        def ag_body(step, carry):
            ag_step(step, step - 2, True, False, chore if steady else None)
            return carry

        lax.fori_loop(3, half - 1, ag_body, 0)
    if half > 3:
        ag_step(half - 1, half - 3, True, True)
    if half < 3:
        weights_in()
    for t in range(LIMIT // 24 * 24, LIMIT):
        plan.send(t)
    plan.finish()
    for p in range(PIECES):
        for way in range(2):
            if shares(way, p):
                landed(way, half, p).wait_recv()
    whole(half)
    done = [g for g in range(half) if not (g <= half - 3)]

    served = [jnp.floor(s / blocks).astype(jnp.int32) for s in plan.held()]

    def factors(at):
        extra = rows_all[at, :, width:].astype(jnp.float32)
        lanes = lax.broadcasted_iota(jnp.int32, (count, tail), 1)
        return [
            jnp.sum(jnp.where((lanes % experts == s) & (lanes < 3 * experts), extra, 0.0), axis=1, keepdims=True)
            for s in served
        ]

    def contribution(h, f, p):
        total = None
        for q in range(2):
            value = lax.dot_general(
                h[q], downs[q, pl.ds(p * cols, cols), :], (((1,), (1,)), ((), ())), preferred_element_type=jnp.float32
            )
            value = f[q] * value
            total = value if total is None else total + value
        return total

    def both(step):
        owners = (around(half - step + 1), around(step - 1 - half))
        h = [jnp.concatenate([hidden[o, q] for o in owners], axis=0) for q in range(2)]
        fs = [factors(o) for o in owners]
        return h, [jnp.concatenate([fs[0][q], fs[1][q]], axis=0) for q in range(2)]

    def send_on(way, step, p):
        return pltpu.make_async_remote_copy(
            src_ref=outbox.at[way, step % 2, p], dst_ref=inbox.at[way, step % 2, p],
            send_sem=rs_send.at[way, step % 2, p], recv_sem=rs_recv.at[way, step % 2, p],
            device_id=ways[way], device_id_type=MESH,
        )

    def rs_step(step, first, second, reuse):
        h, f = both(step)
        for p in range(PIECES):
            value = contribution(h, f, p)
            sent = [way for way in range(2) if not first or shares(way, p)]
            met = [way for way in range(2) if not first and (not second or shares(way, p))]
            for way in met:
                send_on(way, step - 1, p).wait_recv()
            mine = [value[way * count:(way + 1) * count] for way in range(2)]
            for way in met:
                mine[way] = mine[way] + inbox[way, (step - 1) % 2, p].astype(jnp.float32)
            for way in sent:
                if reuse is True or (reuse == "part" and shares(way, p)):
                    send_on(way, step - 2, p).wait_send()
                outbox[way, step % 2, p] = mine[way].astype(jnp.bfloat16)
            for way in sent:
                send_on(way, step, p).start()

    rs_step(1, True, False, False)
    for g in done:
        whole(g)
    if half > 1:
        rs_step(2, False, True, False)
    if half > 2:
        rs_step(3, False, False, "part")
    if half > 3:

        def rs_body(step, carry):
            rs_step(step, False, False, True)
            return carry

        lax.fori_loop(4, half + 1, rs_body, 0)
    for copy in mate_copies():
        copy.wait()
    h = [hidden[chip, q] for q in range(2)]
    f = factors(chip)
    for p in range(PIECES):
        value = contribution(h, f, p)
        for way in range(2):
            send_on(way, half, p).wait_recv()
            value = value + inbox[way, half % 2, p].astype(jnp.float32)
        result[:, pl.ds(p * cols, cols)] = value.astype(jnp.bfloat16)
    for p in range(PIECES):
        for way in range(2):
            for step in range(max(1, half - 1), half + 1):
                if step > 1 or shares(way, p):
                    send_on(way, step, p).wait_send()
            final = half if shares(way, p) else half - 1
            for step in range(max(1, final - 1), final + 1):
                pass_on(way, step, p).wait_send()


def token_layer(old_place, new_place, tokens, ids, logits, gate, up, down, chips, collective_id):
    count, width = tokens.shape
    feats = gate.shape[2]
    cols = width // PIECES
    slots = 2 * chips
    any_space = pl.BlockSpec(memory_space=pl.ANY)
    smem = pl.BlockSpec(memory_space=pltpu.SMEM)
    vmem = pl.BlockSpec(memory_space=pltpu.VMEM)
    dma = pltpu.SemaphoreType.DMA
    weights = [w.reshape(w.shape[1:]) for w in (gate, up, down)]
    return pl.pallas_call(
        functools.partial(token_kernel, chips, EXPERTS, slots // EXPERTS),
        out_shape=(
            jax.ShapeDtypeStruct(tokens.shape, tokens.dtype),
            jax.ShapeDtypeStruct((-(-(LIMIT + 2) // 8) * 8, LANES), jnp.int32),
            jax.ShapeDtypeStruct((1,), jnp.int32),
            jax.ShapeDtypeStruct((3, width // 2, feats), gate.dtype),
        ),
        in_specs=[vmem, vmem, vmem, vmem, vmem, any_space, any_space, any_space],
        out_specs=(vmem, vmem, smem, any_space),
        scratch_shapes=[
            pltpu.VMEM((chips, count, width + LANES), tokens.dtype),
            pltpu.VMEM((2, width, 2 * feats), tokens.dtype),
            pltpu.VMEM((2, width, feats), tokens.dtype),
            pltpu.VMEM((chips, 2, count, feats), tokens.dtype),
            pltpu.VMEM((2, 2, PIECES, count, cols), tokens.dtype),
            pltpu.VMEM((2, 2, PIECES, count, cols), tokens.dtype),
            pltpu.VMEM((4, slots, LANES), jnp.float32),
            pltpu.VMEM((2, slots, LANES), jnp.float32),
            pltpu.VMEM((2, 8, LANES), jnp.float32),
            pltpu.VMEM((2 * LANES, LANES), jnp.float32),
            dma((3,)),
            dma((2, 3)),
            dma((3,)),
            dma((2, 2, PIECES)),
            dma((2, 2, PIECES)),
            dma((2, 2, PIECES)),
            dma((2, 2, PIECES)),
        ],
        compiler_params=pltpu.CompilerParams(
            collective_id=collective_id, has_side_effects=True, vmem_limit_bytes=67043328
        ),
        name="token_layer",
    )(old_place.reshape(1, slots), new_place.reshape(1, slots), tokens, ids.T, logits.T, *weights)


def move_kernel(
    chips, steps, per,
    table, gate, up, down, mate_half,
    new_gate, new_up, new_down,
    pool, landing, sending, stage, load_sems, mate_sem, send_sems, recv_sems, stage_sems, out_sems,
):
    me = lax.axis_index("expert")
    chip, core = me // 2, me % 2
    mate = {"expert": me + 1 - 2 * core}
    above = {"expert": ((chip + 1) % chips) * 2 + core}
    below = {"expert": ((chip + chips - 1) % chips) * 2 + core}
    own_arrays = (gate, up, down)
    new_arrays = (new_gate, new_up, new_down)

    loads = [
        pltpu.make_async_copy(
            array.at[pl.ds(core * per, per)], pool.at[pl.ds(core * PACKETS + a * per, per)], load_sems.at[a]
        )
        for a, array in enumerate(own_arrays)
    ]
    loads.append(pltpu.make_async_copy(mate_half, pool.at[pl.ds((1 - core) * PACKETS, PACKETS)], mate_sem))
    for load in loads:
        load.start()
    barrier = pltpu.get_barrier_semaphore()
    for other in (mate, above, below):
        pl.semaphore_signal(barrier, inc=1, device_id=other, device_id_type=MESH)
    pl.semaphore_wait(barrier, 3)
    for load in loads:
        load.wait()

    def hop(t, way):
        return pltpu.make_async_remote_copy(
            src_ref=sending.at[way, t % SENDS],
            dst_ref=landing.at[way, t % LANDINGS],
            send_sem=send_sems.at[way, t % SENDS],
            recv_sem=recv_sems.at[way, t % LANDINGS],
            device_id=(above, below)[way],
            device_id_type=MESH,
        )

    def take(t):
        for way in range(2):
            hop(t, way).wait_recv()
            pool[2 * PACKETS + 2 * t + way] = landing[way, t % LANDINGS]

    def give(t, free):
        for way in range(2):
            if free:
                hop(t - SENDS, way).wait_send()
            sending[way, t % SENDS] = pool[table[t, way]]
        for way in range(2):
            hop(t, way).start()

    for t in range(SENDS):
        if t >= LAG:
            take(t - LAG)
        give(t, False)

    def body(t, carry):
        take(t - LAG)
        give(t, True)
        return carry

    lax.fori_loop(SENDS, steps, body, 0)
    for t in range(steps - LAG, steps):
        take(t)
    for t in range(steps - SENDS, steps):
        for way in range(2):
            hop(t, way).wait_send()

    def away(p, slot):
        return pltpu.make_async_remote_copy(
            src_ref=stage.at[1, slot],
            dst_ref=new_arrays[p // per].at[core * per + p % per],
            send_sem=out_sems.at[0, slot],
            recv_sem=out_sems.at[1, p],
            device_id=mate,
            device_id_type=MESH,
        )

    def home(p, slot):
        return pltpu.make_async_copy(
            stage.at[0, slot], new_arrays[p // per].at[core * per + p % per], stage_sems.at[slot]
        )

    for p in range(PACKETS):
        slot = p % STAGES
        if p >= STAGES:
            home(p - STAGES, slot).wait()
            away(p - STAGES, slot).wait_send()
        stage[0, slot] = pool[table[LIMIT + core, p]]
        stage[1, slot] = pool[table[LIMIT + 1 - core, p]]
        home(p, slot).start()
        away(p, slot).start()
    for p in range(PACKETS - STAGES, PACKETS):
        home(p, p % STAGES).wait()
        away(p, p % STAGES).wait_send()
    for p in range(PACKETS):
        away(p, p % STAGES).wait_recv()


def move(chips, steps, collective_id, table, gate, up, down, mate_half):
    wide, feats = gate.shape[1], gate.shape[2]
    per = PACKETS // 3
    rows = wide // (2 * per)
    packet = (rows, feats)
    cut = (2 * per, rows, feats)
    any_space = pl.BlockSpec(memory_space=pl.ANY)
    smem = pl.BlockSpec(memory_space=pltpu.SMEM)
    out = jax.ShapeDtypeStruct(cut, gate.dtype)
    dma = pltpu.SemaphoreType.DMA
    moved = pl.pallas_call(
        functools.partial(move_kernel, chips, steps, per),
        out_shape=(out, out, out),
        in_specs=[smem, any_space, any_space, any_space, any_space],
        out_specs=(any_space, any_space, any_space),
        scratch_shapes=[
            pltpu.VMEM((2 * PACKETS + 2 * steps,) + packet, gate.dtype),
            pltpu.VMEM((2, LANDINGS) + packet, gate.dtype),
            pltpu.VMEM((2, SENDS) + packet, gate.dtype),
            pltpu.VMEM((2, STAGES) + packet, gate.dtype),
            dma((3,)),
            dma,
            dma((2, SENDS)),
            dma((2, LANDINGS)),
            dma((STAGES,)),
            dma((2, PACKETS)),
        ],
        compiler_params=pltpu.CompilerParams(
            collective_id=collective_id, has_side_effects=True, vmem_limit_bytes=67043328
        ),
        name="move",
    )(table, gate.reshape(cut), up.reshape(cut), down.reshape(cut), mate_half.reshape((PACKETS,) + packet))
    return tuple(m.reshape(gate.shape) for m in moved)

def in_one_piece(arrays, split_dim, concat_dim):
    both = jnp.concatenate(arrays, axis=2)
    both = lax.all_to_all(both, "expert", split_axis=split_dim, concat_axis=concat_dim, tiled=True)
    return jnp.split(both, len(arrays), axis=2)


def two_exchanges(old_place, new_place, held_gate, held_up, held_down):
    ids = jnp.arange(old_place.shape[0], dtype=jnp.int32)
    slot_at = jnp.sum(jnp.where(new_place[:, None] == ids[None, :], ids[:, None], 0), axis=0)
    source_of = jnp.take(old_place, slot_at)
    bands = in_one_piece((held_gate, held_up, held_down), 1, 0)
    return tuple(in_one_piece([jnp.take(b, source_of, axis=0) for b in bands], 0, 1))


def per_device(
    tokens, route_ids, route_logits, old_place, new_place, held_gate, held_up, held_down
):
    chips = lax.axis_size("expert") // 2
    held = (held_gate, held_up, held_down)
    output, table, choice, mate_half = token_layer(
        old_place, new_place, tokens, route_ids, route_logits, *held, chips, len(STEPS)
    )

    def planned(i, steps, old, new, table, half, *held):
        return move(chips, steps, i, table, *held, half)

    def general(old, new, table, half, *held):
        return two_exchanges(old, new, *held)

    branches = [functools.partial(planned, i, steps) for i, steps in enumerate(STEPS)] + [general]
    moved = lax.switch(choice[0], branches, old_place, new_place, table, mate_half, *held)
    return (output,) + tuple(moved)


def solution(mesh):
    placed = (
        P(("groups", "expert"), None),
        P(("groups", "expert"), None),
        P(("groups", "expert"), None),
        P(),
        P(),
        P(("groups", "expert"), None, None),
        P(("groups", "expert"), None, None),
        P(("groups", "expert"), None, None),
    )
    return jax.shard_map(
        per_device,
        mesh=mesh,
        in_specs=placed,
        out_specs=(
            P(("groups", "expert"), None),
            P(("groups", "expert"), None, None),
            P(("groups", "expert"), None, None),
            P(("groups", "expert"), None, None),
        ),
        check_vma=False,
    )
```

time: 2050 us -> 717 us (0.35)
  waiting for transfers between devices: 1680 us -> 0 us
  Pallas kernels: 0 us -> 692 us
  local copies, waits for them, and re-layouts: 167 us -> 7.51 us
  other arithmetic: 118 us -> 0 us
  starting transfers between devices: 57.6 us -> 0 us
    all_to_all x4 -> x0, waiting for transfers between devices: 1680 us -> none  [the longest x2 809 us: in_one_piece(): lax.all_to_all(both, axis, split_axis=split_dim, concat_axis=concat_dim,...]
    pallas_call x0 -> x2, Pallas kernels: none -> 692 us  [the longest x1 524 us: move(): pl.pallas_call(functools.partial(move_kernel, chips, steps, per), out_sha...]
    unnamed x1 -> x0, other arithmetic: 102 us -> none
    concatenate x1 -> x0, local copies, waits for them, and re-layouts: 88.7 us -> none  [in_one_piece(): both = jnp.concatenate(arrays, axis=along)]
    all_to_all x4 -> x0, starting transfers between devices: 57.6 us -> none  [the longest x1 35.1 us: per_device(): lax.all_to_all(outgoing, 'expert', split_axis=0, concat_axis=0, tiled=True)]
    unnamed x21 -> x8, local copies, waits for them, and re-layouts: 41.2 us -> 7.51 us
  transfers between devices with their start and end apart: 4 -> 0, of which waited for: 4 -> 0; matrix products, arithmetic and copies ran while one was open for 14% -> 0% of each run, Pallas kernels for 0% -> 0%
where the time goes in v1:
time: 717 us; the launch traced here: 704 us
  Pallas kernels  692 us (97%)
  local copies, waits for them, and re-layouts  7.51 us (1%)
    pallas_call x1, Pallas kernels, move(): pl.pallas_call(functools.partial(move_kernel, chips, steps, per), out_sha...  524 us
    pallas_call x1, Pallas kernels, token_layer(): pl.pallas_call(functools.partial(token_kernel, chips, EXPERTS, slots // E...  168 us

profile of v1, /device:TPU:46, one launch (start us, length us, event | category | flops | bytes accessed | tf_op | source)
XLA Modules:
  0.0 704.0 jit_solution(16988367783877195594)
XLA Ops:
  0.6 167.9 %token_layer.1 = (bf16[16,6144]{1,0:T(8,128)(2,1)}, s32[152,128]{1,0:T(8,128)}, s32[1]{0:T(128)}, bf16[3,3072,128]{2,1,0:T(8,128)(2,1)}) custom-call(s32[1,64]{1,0:T(1,128)} %bitcast.66, s32[1,64]{1,0:T(1,128)} %bitcast.124, bf16[16,6144]{1,0:T(8,128)(2,1)} %tokens.1, s32[2,16]{1,0:T(2,128)} %bitcast.122, f32[2,16]{1,0:T(2,128)} %bitcast.123, ...), custom_call_target="tpu_custom_call" | custom-call | tf_op jit(solution)/shard_map/token_layer/pallas_call | solution.py:526
  169.1 527.4 %conditional.1 = (bf16[1,6144,128]{2,1,0:T(8,128)(2,1)}, bf16[1,6144,128]{2,1,0:T(8,128)(2,1)}, bf16[1,6144,128]{2,1,0:T(8,128)(2,1)}) conditional(s32[]{:T(128)} %bitcast.59, (bf16[1,6144,128]{2,1,0:T(8,128)(2,1)}, bf16[1,6144,128]{2,1,0:T(8,128)(2,1)}, bf16[1,6144,128]{2,1,0:T(8,128)(2,1)}, ...), branch_computations={%region_0.0_spmd, %region_1.0_spmd, %region_2.0_spmd, %region_3.0_... | conditional | flops 30686144 | bytes 139999296 | solution.py:727
  171.9 524.1 %move.10 = (bf16[8,768,128]{2,1,0:T(8,128)(2,1)}, bf16[8,768,128]{2,1,0:T(8,128)(2,1)}, bf16[8,768,128]{2,1,0:T(8,128)(2,1)}) custom-call(s32[152,128]{1,0:T(8,128)} %get-tuple-element.105.table, bf16[8,768,128]{2,1,0:T(8,128)(2,1)} %bitcast.71, bf16[8,768,128]{2,1,0:T(8,128)(2,1)} %bitcast.79, bf16[8,768,128]{2,1,0:T(8,128)(2,1)} %bitcast.87, ...), custom_call_target="tpu_custom_call" | custom-call | tf_op jit(solution)/shard_map/cond/branch_3_fun/move/pallas_call | solution.py:673
  696.5 1.6 copy.53
  698.1 0.0 copy-start.3
  698.1 2.8 copy.54
  700.9 0.0 copy-done.3
  700.9 0.0 copy-start.4
  700.9 1.1 copy.55
  702.0 0.8 copy-done.4
  702.9 1.1 copy.56
Async XLA Ops:
  698.1 2.8 copy-start.3
  700.9 2.0 copy-start.4
